TPU v7x, 32 devices: a whole 2x2x4 slice. The times are simulated.
32 devices in a mesh: dp: 4 (over x, y), tp: 8 (over z, core).
Axes of the slice: x: 2, y: 2, z: 4, core: 2. Of those that a mesh axis runs over, the one named last changes fastest.
Arguments:
- x: bfloat16 [8, 512, 4096], P('dp', 'tp'), parts along dimension 0
- k_cache: bfloat16 [8, 4096, 32, 128], P('dp', None, 'tp'), parts along dimension 0
- v_cache: bfloat16 [8, 4096, 32, 128], P('dp', None, 'tp'), parts along dimension 0
- prefix_len: int32 [8], P('dp'), parts along dimension 0
- valid_len: int32 [8], P('dp'), parts along dimension 0
- g_attn: bfloat16 [4096], replicated
- w_q: bfloat16 [4096, 4096], P(None, 'tp')
- b_q: bfloat16 [4096], P('tp')
- w_k: bfloat16 [4096, 4096], P(None, 'tp')
- b_k: bfloat16 [4096], P('tp')
- w_v: bfloat16 [4096, 4096], P(None, 'tp')
- b_v: bfloat16 [4096], P('tp')
- w_o: bfloat16 [4096, 4096], P('tp')
- g_mlp: bfloat16 [4096], replicated
- w_gate: bfloat16 [4096, 11008], P(None, 'tp')
- w_up: bfloat16 [4096, 11008], P(None, 'tp')
- w_down: bfloat16 [11008, 4096], P('tp')
Outputs:
- output 1: bfloat16 [8, 512, 4096], P('dp', 'tp'), parts along dimension 0
- output 2: bfloat16 [8, 4096, 32, 128], P('dp', None, 'tp'), parts along dimension 0
- output 3: bfloat16 [8, 4096, 32, 128], P('dp', None, 'tp'), parts along dimension 0
There are 4 independent parts. A program takes and returns all parts, laid end to end along the dimension named above; an argument that names none is the same for every part.
All inputs are finite; a program needn't handle non-finite values.
Results may differ from a plain program's by a relative error of at most 0.0176057.
Values are sent between devices in bfloat16 or wider.
A program may use at most 1 GiB of HBM per device.

v0:
```python
import jax
import jax.numpy as jnp
from jax import lax
from jax.sharding import PartitionSpec as P

ROPE_THETA = 1.0e6
NORM_EPS = 1.0e-6


def rms_norm(hidden, gain):
    wide_vals = hidden.astype(jnp.float32)
    inv_rms = lax.rsqrt(jnp.mean(wide_vals * wide_vals, axis=-1, keepdims=True) + NORM_EPS)
    return (wide_vals * inv_rms * gain.astype(jnp.float32)).astype(jnp.bfloat16)


def rotate_heads(heads, positions):
    half = heads.shape[-1] // 2
    inv_freq = ROPE_THETA ** (-(jnp.arange(half, dtype=jnp.float32) * 2.0) / heads.shape[-1])
    angles = positions.astype(jnp.float32)[..., None] * inv_freq
    cos_t = jnp.cos(angles)[..., None, :]
    sin_t = jnp.sin(angles)[..., None, :]
    wide = heads.astype(jnp.float32)
    first_half = wide[..., :half]
    second_half = wide[..., half:]
    rotated = jnp.concatenate([first_half * cos_t - second_half * sin_t, second_half * cos_t + first_half * sin_t], axis=-1)
    return rotated.astype(jnp.bfloat16)


def project(hidden, weight, bias):
    total = jnp.einsum("rcd,dn->rcn", hidden, weight, preferred_element_type=jnp.float32)
    return (total + bias.astype(jnp.float32)).astype(jnp.bfloat16)


def write_rows(cache, new_rows, prefix, valid):
    n_tokens = new_rows.shape[1]
    row_ids = jnp.arange(n_tokens, dtype=jnp.int32)[None, :, None, None]
    window = (1, n_tokens, cache.shape[2], cache.shape[3])

    def body(req_idx, buffer):
        start = prefix[req_idx]
        old_rows = lax.dynamic_slice(buffer, (req_idx, start, 0, 0), window)
        fresh = lax.dynamic_slice_in_dim(new_rows, req_idx, 1, axis=0)
        merged = jnp.where(row_ids < valid[req_idx], fresh, old_rows)
        return lax.dynamic_update_slice(buffer, merged, (req_idx, start, 0, 0))

    return lax.fori_loop(0, cache.shape[0], body, cache)


def attend(queries, k_cache, v_cache, prefix, valid):
    n_req, n_tokens, q_heads, head_dim = queries.shape
    slots, kv_local = k_cache.shape[1], k_cache.shape[2]
    query_groups = queries.reshape(n_req, n_tokens, kv_local, q_heads // kv_local, head_dim)
    scores = jnp.einsum("rckgd,rskd->rkgcs", query_groups, k_cache, preferred_element_type=jnp.float32) * (head_dim ** -0.5)
    row_ids = jnp.arange(n_tokens, dtype=jnp.int32)
    limit = prefix[:, None] + jnp.minimum(row_ids[None, :], valid[:, None] - 1)
    visible = jnp.arange(slots, dtype=jnp.int32)[None, None, :] <= limit[:, :, None]
    scores = jnp.where(visible[:, None, None], scores, -1.0e30)
    attn_probs = jax.nn.softmax(scores, axis=-1).astype(jnp.bfloat16)
    mixed = jnp.einsum("rkgcs,rskd->rckgd", attn_probs, v_cache, preferred_element_type=jnp.float32)
    return mixed.astype(jnp.bfloat16).reshape(n_req, n_tokens, q_heads * head_dim)


def attention_heads(normed_full, k_cache, v_cache, prefix, valid, w_q, b_q, w_k, b_k, w_v, b_v):
    n_req, n_tokens = normed_full.shape[0], normed_full.shape[1]
    head_dim = k_cache.shape[-1]
    positions = prefix[:, None] + jnp.arange(n_tokens, dtype=jnp.int32)[None, :]
    queries = rotate_heads(project(normed_full, w_q, b_q).reshape(n_req, n_tokens, -1, head_dim), positions)
    keys_new = rotate_heads(project(normed_full, w_k, b_k).reshape(n_req, n_tokens, -1, head_dim), positions)
    values_new = project(normed_full, w_v, b_v).reshape(n_req, n_tokens, -1, head_dim)
    k_out = write_rows(k_cache, keys_new, prefix, valid)
    v_out = write_rows(v_cache, values_new, prefix, valid)
    return attend(queries, k_out, v_out, prefix, valid), k_out, v_out


def mlp_partial(normed_full, w_gate, w_up, w_down):
    gate = jnp.einsum("rcd,df->rcf", normed_full, w_gate, preferred_element_type=jnp.float32)
    up_proj = jnp.einsum("rcd,df->rcf", normed_full, w_up, preferred_element_type=jnp.float32)
    hidden_act = (jax.nn.silu(gate) * up_proj).astype(jnp.bfloat16)
    return jnp.einsum("rcf,fd->rcd", hidden_act, w_down, preferred_element_type=jnp.float32).astype(jnp.bfloat16)


def add_rounded(first, second):
    return (first.astype(jnp.float32) + second.astype(jnp.float32)).astype(jnp.bfloat16)


def solution(mesh):
    row_spec = P("dp", "tp", None)
    cache_spec = P("dp", None, "tp", None)
    req_spec = P("dp")
    rep_spec = P(None)
    col_spec = P(None, "tp")
    bias_spec = P("tp")
    down_spec = P("tp", None)

    def layer(x_rows, k_cache, v_cache, prefix, valid, g_attn, w_q, b_q, w_k, b_k, w_v, b_v, w_o, g_mlp, w_gate, w_up, w_down):
        normed = rms_norm(x_rows, g_attn)
        normed_full = lax.all_gather(normed, "tp", axis=1, tiled=True)
        attended, k_out, v_out = attention_heads(normed_full, k_cache, v_cache, prefix, valid, w_q, b_q, w_k, b_k, w_v, b_v)
        attn_part = jnp.einsum("rcn,nd->rcd", attended, w_o, preferred_element_type=jnp.float32).astype(jnp.bfloat16)
        attn_rows = lax.psum_scatter(attn_part, "tp", scatter_dimension=1, tiled=True)
        resid_mid = add_rounded(x_rows, attn_rows)
        normed_mlp = rms_norm(resid_mid, g_mlp)
        mlp_full = lax.all_gather(normed_mlp, "tp", axis=1, tiled=True)
        down_part = mlp_partial(mlp_full, w_gate, w_up, w_down)
        down_rows = lax.psum_scatter(down_part, "tp", scatter_dimension=1, tiled=True)
        return add_rounded(resid_mid, down_rows), k_out, v_out

    in_specs = (row_spec, cache_spec, cache_spec, req_spec, req_spec, rep_spec, col_spec, bias_spec, col_spec, bias_spec, col_spec, bias_spec, down_spec, rep_spec, col_spec, col_spec, down_spec)
    return jax.shard_map(layer, mesh=mesh, in_specs=in_specs, out_specs=(row_spec, cache_spec, cache_spec), check_vma=False)
```

profile of v0, /device:TPU:0, one launch (start us, length us, event | category | flops | bytes accessed | tf_op | source)
XLA Modules:
  0.0 600.4 jit_solution(10279667574969703825)
XLA Ops:
  7.2 0.0 all-gather.3.cloned.1.call-start
  7.2 9.1 %copy.91 = bf16[2,4096,4,128]{3,2,1,0:T(4,128)(2,1)} copy(bf16[2,4096,4,128]{3,2,1,0:T(4,128)(2,1)} %param.22) | data formatting | bytes 16777216
  16.3 0.0 copy-start.6
  16.3 0.0 copy-start.7
  16.4 0.0 copy-start.9
  16.4 3.4 copy.92
  19.8 0.3 fusion.30
  20.1 1.3 fusion.32
  21.4 0.0 all-gather.3.cloned.1.call-update
  21.4 0.0 reduce-scatter.3.cloned.1.call-start
  21.6 0.1 minimum_add_fusion
  21.6 3.0 multiply_cosine_fusion
  24.7 5.3 iota_compare_fusion
  30.0 75.8 %all-gather.3.cloned.1.call-done = bf16[2,512,4096]{2,1,0:T(8,128)(2,1)} async-done(((bf16[2,64,4096]{2,1,0:T(8,128)(2,1)}), bf16[2,512,4096]{2,1,0:T(8,128)(2,1)}) %all-gather.3.cloned.1.call-update) | async-done | bytes 8388624 | tf_op jit(solution)/shard_map/all_gather | solution.py:97
  105.8 9.1 %add_convert_fusion.3 = bf16[2,512,512]{1,2,0:T(8,128)(2,1)S(1)} fusion(bf16[2,512,4096]{2,1,0:T(8,128)(2,1)} %all-gather.3.cloned.1.call-done, bf16[4096,512]{1,0:T(8,128)(2,1)} %param.29, f32[512]{0:T(512)S(1)} %convert_element_type.100), kind=kOutput, calls=%fused_computation.55 | convolution fusion | flops 4296015872 | bytes 13633536 | tf_op jit(solution)/shard_map/rcd,dn->rcn/dot_general | solution.py:30
  114.9 1.2 fusion.56
  116.1 1.8 copy.57
  118.0 9.5 %add_convert_fusion.1 = bf16[2,512,512]{1,2,0:T(8,128)(2,1)S(1)} fusion(bf16[2,512,4096]{2,1,0:T(8,128)(2,1)} %all-gather.3.cloned.1.call-done, bf16[4096,512]{1,0:T(8,128)(2,1)} %param.27, f32[512]{0:T(512)S(1)} %convert_element_type.105), kind=kOutput, calls=%fused_computation.52 | convolution fusion | flops 4296015872 | bytes 13633536 | tf_op jit(solution)/shard_map/rcd,dn->rcn/dot_general | solution.py:30
  127.4 1.7 fusion.55
  129.1 3.2 copy.59
  132.3 3.2 copy.58
  135.5 1.9 copy.56
  137.4 5.3 subtract_convert_fusion
  142.7 0.6 pad_maximum_fusion
  143.3 19.1 %while.29 = (s32[]{:T(128)}, bf16[2,4096,4,128]{3,2,1,0:T(4,128)(2,1)}, s32[2]{0:T(128)S(1)}, bf16[2,512,4,128]{3,1,2,0:T(8,128)(2,1)S(1)}, s32[2]{0:T(128)S(1)}, /*index=5*/s32[]{:T(128)}, s32[]{:T(128)}, s32[]{:T(128)}) while((s32[]{:T(128)}, bf16[2,4096,4,128]{3,2,1,0:T(4,128)(2,1)}, s32[2]{0:T(128)S(1)}, ...), condition=%wide.region_4.5_spmd.clone, body=%wide.region_3.4_spmd.clone.sunk | while | flops 262661 | bytes 2622631 | solution.py:46
  143.3 0.6 dynamic_slice.83
  144.0 0.6 dynamic_slice.82
  146.2 0.6 compare_reduce_fusion.5
  146.9 5.9 fusion.65
  152.8 0.6 dynamic_slice.83
  153.5 0.6 dynamic_slice.82
  155.7 0.6 compare_reduce_fusion.5
  156.4 5.9 fusion.65
  162.4 9.1 %add_convert_fusion.4 = bf16[2,512,512]{1,2,0:T(8,128)(2,1)S(1)} fusion(bf16[2,512,4096]{2,1,0:T(8,128)(2,1)} %all-gather.3.cloned.1.call-done, bf16[4096,512]{1,0:T(8,128)(2,1)} %param.31, f32[512]{0:T(512)S(1)} %convert_element_type.98), kind=kOutput, calls=%fused_computation.56 | convolution fusion | flops 4296015872 | bytes 13633536 | tf_op jit(solution)/shard_map/rcd,dn->rcn/dot_general | solution.py:30
  171.5 14.7 %while.28 = (s32[]{:T(128)}, bf16[2,4096,4,128]{3,2,1,0:T(4,128)(2,1)}, s32[2]{0:T(128)S(1)}, bf16[2,512,4,128]{1,3,2,0:T(8,128)(2,1)S(1)}, s32[2]{0:T(128)S(1)}, /*index=5*/s32[]{:T(128)}, s32[]{:T(128)}, s32[]{:T(128)}) while((s32[]{:T(128)}, bf16[2,4096,4,128]{3,2,1,0:T(4,128)(2,1)}, s32[2]{0:T(128)S(1)}, ...), condition=%wide.region_2.3_spmd.clone, body=%wide.region_1.2_spmd.clone.sunk | while | flops 262661 | bytes 3671207 | solution.py:46
  171.5 0.6 dynamic_slice.79
  172.1 0.6 dynamic_slice.78
  174.6 0.6 compare_reduce_fusion.4
  175.2 0.3 copy.73
  175.5 3.3 select_dynamic-update-slice_fusion.2
  178.8 0.6 dynamic_slice.79
  179.4 0.6 dynamic_slice.78
  181.9 0.6 compare_reduce_fusion.4
  182.6 0.3 copy.73
  182.9 3.3 select_dynamic-update-slice_fusion.2
  186.2 29.7 %fusion.6 = (f32[2,4,512]{2,1,0:T(4,128)S(1)}, f32[2,4,4096,512]{3,2,1,0:T(8,128)}) fusion(pred[2,512,4096]{1,2,0:T(8,128)(4,1)} %iota_compare_fusion, bf16[2,512,4,64]{3,1,2,0:T(8,128)(2,1)} %get-tuple-element.288, bf16[2,512,4,64]{3,1,2,0:T(8,128)(2,1)S(1)} %get-tuple-element.287, bf16[2,4096,4,128]{3,2,1,0:T(4,128)(2,1)} %get-tuple-element.219), kind=kOutput, calls=%fused_computation.13 | convolution fusion | flops 4347392000 | bytes 80756736 | tf_op jit(solution)/shard_map/rckgd,rskd->rkgcs/dot_general | solution.py:53
  215.9 22.7 %fusion.5 = f32[2,4,512]{2,1,0:T(4,128)S(1)} fusion(f32[2,4,4096,512]{3,2,1,0:T(8,128)} %get-tuple-element.302, f32[2,4,512]{2,1,0:T(4,128)S(1)} %get-tuple-element.301, pred[2,512,4096]{1,2,0:T(8,128)(4,1)} %iota_compare_fusion), kind=kLoop, calls=%fused_computation.12 | loop fusion | flops 67104768 | bytes 71335936 | tf_op jit(solution)/shard_map/reduce_sum | solution.py:58
  238.6 29.8 %fusion.44 = bf16[2,4,128,512]{3,2,1,0:T(8,128)(2,1)S(1)} fusion(f32[2,4,512]{2,1,0:T(4,128)S(1)} %fusion.5, f32[2,4,512]{2,1,0:T(4,128)S(1)} %get-tuple-element.301, f32[2,4,4096,512]{3,2,1,0:T(8,128)} %get-tuple-element.302, pred[2,512,4096]{1,2,0:T(8,128)(4,1)} %iota_compare_fusion, bf16[2,4096,4,128]{3,2,1,0:T(4,128)(2,1)} %get-tuple-element.220), kind=kOutput, calls=%fused_computation.57 | convolution fusion | flops 4379377664 | bytes 80773120 | tf_op jit(solution)/shard_map/rkgcs,rskd->rckgd/dot_general | solution.py:59
  268.4 9.0 %convolution_convert_fusion = bf16[2,512,4096]{2,1,0:T(8,128)(2,1)} fusion(bf16[2,512,512]{1,2,0:T(8,128)(2,1)S(1)} %bitcast.85, bf16[512,4096]{1,0:T(8,128)(2,1)} %param.33), kind=kOutput, calls=%fused_computation.27 | convolution fusion | flops 4299161600 | bytes 13631488 | tf_op jit(solution)/shard_map/rcn,nd->rcd/dot_general | solution.py:99
  277.4 0.0 reduce-scatter.3.cloned.1.call-update
  277.4 0.0 all-gather.5.cloned.1.call-start
  277.5 0.6 copy-done.5
  278.1 87.7 %reduce-scatter.3.cloned.1.call-done = bf16[2,64,4096]{2,1,0:T(8,128)(2,1)} async-done(((bf16[2,512,4096]{2,1,0:T(8,128)(2,1)}), bf16[2,64,4096]{2,1,0:T(8,128)(2,1)}) %reduce-scatter.3.cloned.1.call-update) | async-done | bytes 1048592 | tf_op jit(solution)/shard_map/reduce_scatter | solution.py:100
  365.8 1.7 fusion.34
  367.5 2.6 fusion.36
  370.1 0.0 all-gather.5.cloned.1.call-update
  370.1 0.0 reduce-scatter.5.cloned.1.call-start
  370.1 80.3 %all-gather.5.cloned.1.call-done = bf16[2,512,4096]{2,1,0:T(8,128)(2,1)} async-done(((bf16[2,64,4096]{2,1,0:T(8,128)(2,1)}), bf16[2,512,4096]{2,1,0:T(8,128)(2,1)}) %all-gather.5.cloned.1.call-update) | async-done | bytes 8388624 | tf_op jit(solution)/shard_map/all_gather | solution.py:103
  450.4 18.5 %fusion.13 = f32[2,512,1376]{1,2,0:T(8,128)} fusion(bf16[2,512,4096]{2,1,0:T(8,128)(2,1)} %all-gather.5.cloned.1.call-done, bf16[4096,1376]{0,1:T(8,128)(2,1)} %param.35), kind=kOutput, calls=%fused_computation.21 | convolution fusion | flops 11542724608 | bytes 25296896 | tf_op jit(solution)/shard_map/rcd,df->rcf/dot_general | solution.py:76
  468.9 18.0 %multiply_convert_fusion = bf16[2,512,1376]{1,2,0:T(8,128)(2,1)S(1)} fusion(f32[2,512,1376]{1,2,0:T(8,128)} %fusion.13, bf16[2,512,4096]{2,1,0:T(8,128)(2,1)} %all-gather.5.cloned.1.call-done, bf16[4096,1376]{0,1:T(8,128)(2,1)} %param.36), kind=kOutput, calls=%fused_computation.28 | convolution fusion | flops 11551178752 | bytes 28114944 | tf_op jit(solution)/shard_map/rcd,df->rcf/dot_general | solution.py:77
  487.0 15.4 %fusion.18 = bf16[2,512,4096]{2,1,0:T(8,128)(2,1)} fusion(bf16[2,512,1376]{1,2,0:T(8,128)(2,1)S(1)} %multiply_convert_fusion, bf16[1376,4096]{1,0:T(8,128)(2,1)S(1)} %bitcast.84), kind=kOutput, calls=%fused_computation.26 | convolution fusion | flops 11546918912 | bytes 22478848 | tf_op jit(solution)/shard_map/rcf,fd->rcd/dot_general | solution.py:79
  502.4 0.0 reduce-scatter.5.cloned.1.call-update
  502.4 88.4 %reduce-scatter.5.cloned.1.call-done = bf16[2,64,4096]{2,1,0:T(8,128)(2,1)} async-done(((bf16[2,512,4096]{2,1,0:T(8,128)(2,1)}), bf16[2,64,4096]{2,1,0:T(8,128)(2,1)}) %reduce-scatter.5.cloned.1.call-update) | async-done | bytes 1048592 | tf_op jit(solution)/shard_map/reduce_scatter | solution.py:105
  590.8 2.7 fusion.37
  (38 shorter events, 0.3 us)
Async XLA Ops:
  7.2 98.6 %all-gather.3.cloned.1.call-start = ((), (), s32[]{:S(2)}) async-start(), calls=%async_computation.2 | async-start | bytes 9437184 | tf_op jit(solution)/shard_map/all_gather | solution.py:97
  7.2 9.1 %copy-start.3 = (bf16[2,4096,4,128]{3,2,1,0:T(4,128)(2,1)S(1)}, bf16[2,4096,4,128]{3,2,1,0:T(4,128)(2,1)}, u32[]{:S(2)}) copy-start(bf16[2,4096,4,128]{3,2,1,0:T(4,128)(2,1)} %param.23) | copy-start | bytes 25165828
  16.3 3.5 copy-start
  16.3 3.8 copy-start.4
  16.3 5.2 copy-start.6
  16.3 5.2 copy-start.7
  16.3 5.2 copy-start.8
  16.3 5.2 copy-start.10
  16.4 5.2 copy-start.9
  21.4 344.4 %reduce-scatter.3.cloned.1.call-start = ((), (), s32[]{:S(2)}) async-start(), calls=%async_computation.3 | async-start | bytes 9437184 | tf_op jit(solution)/shard_map/reduce_scatter | solution.py:100
  277.4 0.7 copy-start.5
  277.4 88.4 %copy-start.1 = (bf16[2,64,4096]{2,1,0:T(8,128)(2,1)S(1)}, bf16[2,64,4096]{2,1,0:T(8,128)(2,1)}, u32[]{:S(2)}) copy-start(bf16[2,64,4096]{2,1,0:T(8,128)(2,1)} %param.21) | copy-start | bytes 3145732
  277.4 173.0 %all-gather.5.cloned.1.call-start = ((), (), s32[]{:S(2)}) async-start(), calls=%async_computation.4 | async-start | bytes 9437184 | tf_op jit(solution)/shard_map/all_gather | solution.py:103
  370.1 220.7 %reduce-scatter.5.cloned.1.call-start = ((), (), s32[]{:S(2)}) async-start(), calls=%async_computation.5 | async-start | bytes 9437184 | tf_op jit(solution)/shard_map/reduce_scatter | solution.py:105
  450.4 36.5 %slice-start = ((s8[11272192]{0:T(1024)(128)(4,1)}), s8[4194304]{0:T(1024)(128)(4,1)S(1)}, s32[]{:S(2)}) async-start(s8[11272192]{0:T(1024)(128)(4,1)} %bitcast.83), calls=%async_computation.6 | async-start | bytes 8388608
  450.4 36.5 %slice-start.1 = ((s8[11272192]{0:T(1024)(128)(4,1)}), s8[4194304]{0:T(1024)(128)(4,1)S(1)}, s32[]{:S(2)}) async-start(s8[11272192]{0:T(1024)(128)(4,1)} %bitcast.83), calls=%async_computation.7 | async-start | bytes 8388608
  468.9 18.0 %slice-start.2 = ((s8[11272192]{0:T(1024)(128)(4,1)}), s8[2883584]{0:T(1024)(128)(4,1)S(1)}, s32[]{:S(2)}) async-start(s8[11272192]{0:T(1024)(128)(4,1)} %bitcast.83), calls=%async_computation.8 | async-start | bytes 5767168
  502.4 88.4 %copy-start.2 = (bf16[2,64,4096]{2,1,0:T(8,128)(2,1)S(1)}, bf16[2,64,4096]{2,1,0:T(8,128)(2,1)}, u32[]{:S(2)}) copy-start(bf16[2,64,4096]{2,1,0:T(8,128)(2,1)} %reduce-scatter.3.cloned.1.call-done) | copy-start | bytes 3145732
Sparse Core Ops, SparseCore 0:
  21.5 84.1 all-gather.2
  277.5 88.2 reduce-scatter.2
  370.2 80.1 all-gather.4
  502.5 88.2 reduce-scatter.4
where the time goes:
time: 611 us; the launch traced here: 600 us
  waiting for transfers between devices  332 us (54%)
  matrix products  148 us (24%)
  other arithmetic  66.5 us (11%)
  local copies, waits for them, and re-layouts  31.9 us (5%)
  between operations  14.4 us (2%)
  loops' own time  7.23 us (1%)
    reduce_scatter x1, waiting for transfers between devices, layer(): lax.psum_scatter(down_part, 'tp', scatter_dimension=1, tiled=True)  88.4 us
    reduce_scatter x1, waiting for transfers between devices, layer(): lax.psum_scatter(attn_part, 'tp', scatter_dimension=1, tiled=True)  87.7 us
    all_gather x1, waiting for transfers between devices, layer(): mlp_full = lax.all_gather(normed_mlp, 'tp', axis=1, tiled=True)  80.3 us
    all_gather x1, waiting for transfers between devices, layer(): normed_full = lax.all_gather(normed, 'tp', axis=1, tiled=True)  75.8 us
    dot_general x1, matrix products, attend(): jnp.einsum('rkgcs,rskd->rckgd', attn_probs, v_cache, preferred_element_ty...  29.8 us
    dot_general x1, matrix products, attend(): jnp.einsum('rckgd,rskd->rkgcs', query_groups, k_cache, preferred_element_...  29.7 us
    dot_general x3, matrix products, project(): jnp.einsum('rcd,dn->rcn', hidden, weight, preferred_element_type=jnp.floa...  27.7 us
    unnamed x34, local copies, waits for them, and re-layouts  23.3 us
  transfers between devices with their start and end apart: 4, of which 4 were waited for; matrix products, arithmetic and copies ran while one was open for 1% of the time, Pallas kernels for 0%

commit v1 on v0

v1 whole, which is shorter than its diff:
```python
import functools

import jax
import jax.numpy as jnp
from jax import lax
from jax.experimental import pallas as pl
from jax.experimental.pallas import tpu as pltpu
from jax.sharding import PartitionSpec as P

ROPE_THETA = 1.0e6
NORM_EPS = 1.0e-6
MESH = pl.DeviceIdType.MESH
BF = jnp.bfloat16
F32 = jnp.float32

REQ = 2
ROWS = 64
RANKS = 8
CHUNK = ROWS * RANKS
DIM = 4096
HEADS = 4
HD = 128
SLOTS = 4096
OLD = SLOTS - CHUNK
FFN = 1376


class Place:
    def __init__(self):
        t = lax.axis_index("tp")
        self.me = t
        self.c = t % 2
        self.z = t // 2
        self.half = self.z // 2
        self.zm = self.z + self.half * (3 - 2 * self.z)
        self.away = 2 * (self.z + 1 - 2 * self.half) + self.c
        self.near = 2 * (self.z - 1 + 2 * self.half) + self.c
        self.partner = 2 * self.z + 1 - self.c

    def chip(self, dm):
        return dm + self.half * (3 - 2 * dm)

    def blk(self, dm):
        return 2 * self.chip(dm) + self.c

    def other(self, dm):
        return 2 * self.chip(dm) + 1 - self.c

    def outer(self):
        return self.zm == 0

    def inner(self):
        return self.zm == 1


def entry_barrier(pos):
    bar = pltpu.get_barrier_semaphore()

    def signal(dev):
        pl.semaphore_signal(bar, inc=1, device_id={"tp": dev}, device_id_type=MESH)

    signal(pos.partner)
    signal(pos.away)

    @pl.when(pos.inner())
    def _():
        signal(pos.near)
        pl.semaphore_wait(bar, 3)

    @pl.when(pos.outer())
    def _():
        pl.semaphore_wait(bar, 2)


class Gather:
    def __init__(self, pos, buf, send, recv):
        self.pos, self.buf, self.send, self.recv = pos, buf, send, recv

    def copy(self, t, dev, n):
        ref = self.buf.at[t]
        return pltpu.make_async_remote_copy(
            src_ref=ref, dst_ref=ref, send_sem=self.send.at[n], recv_sem=self.recv.at[t],
            device_id={"tp": dev}, device_id_type=MESH)

    def wait_block(self, t):
        self.copy(t, self.pos.partner, 0).wait_recv()

    def start(self, outer=True, inner=True):
        p = self.pos
        if outer:
            @pl.when(p.outer())
            def _():
                self.copy(p.me, p.away, 0).start()
                self.copy(p.me, p.partner, 1).start()
        if inner:
            @pl.when(p.inner())
            def _():
                self.copy(p.me, p.near, 0).start()
                self.copy(p.me, p.away, 1).start()
                self.copy(p.me, p.partner, 2).start()

    def step(self, i):
        p = self.pos

        @pl.when(p.outer())
        def _():
            t = p.blk(i)
            self.wait_block(t)
            self.copy(t, p.partner, 1 + i).start()

        if i == 1:
            @pl.when(p.inner())
            def _():
                t = p.blk(0)
                self.wait_block(t)
                self.copy(t, p.away, 3).start()
                self.copy(t, p.partner, 4).start()
                t = p.blk(2)
                self.wait_block(t)
                self.copy(t, p.near, 5).start()
                self.copy(t, p.partner, 6).start()
        if i == 2:
            @pl.when(p.inner())
            def _():
                t = p.blk(3)
                self.wait_block(t)
                self.copy(t, p.near, 7).start()
                self.copy(t, p.partner, 8).start()

    def finish(self):
        for dm in range(4):
            self.wait_block(self.pos.other(dm))

    def drain(self):
        p = self.pos

        @pl.when(p.outer())
        def _():
            for n in range(5):
                self.copy(p.me, p.partner, n).wait_send()

        @pl.when(p.inner())
        def _():
            for n in range(9):
                self.copy(p.me, p.partner, n).wait_send()


def row_loop(body):
    def run(i, carry):
        body(pl.ds(pl.multiple_of(i * 16, 16), 16))
        return carry

    lax.fori_loop(0, ROWS // 16, run, 0)


class Scatter:
    def __init__(self, pos, part, prx, near, far, psend, precv, send, nrecv, frecv):
        self.pos, self.part, self.prx, self.near, self.far = pos, part, prx, near, far
        self.psend, self.precv, self.send, self.nrecv, self.frecv = psend, precv, send, nrecv, frecv

    def to_partner(self, dm):
        p = self.pos
        return pltpu.make_async_remote_copy(
            src_ref=self.part.at[p.other(dm)], dst_ref=self.prx.at[dm], send_sem=self.psend.at[dm],
            recv_sem=self.precv.at[dm], device_id={"tp": p.partner}, device_id_type=MESH)

    def hop(self, dm, dev, dst, recv):
        return pltpu.make_async_remote_copy(
            src_ref=self.part.at[self.pos.blk(dm)], dst_ref=dst, send_sem=self.send.at[dm],
            recv_sem=recv, device_id={"tp": dev}, device_id_type=MESH)

    def hop_near(self, dm, dev):
        return self.hop(dm, dev, self.near.at[dm - 1], self.nrecv.at[dm - 1])

    def hop_far(self, dm, dev, slot):
        return self.hop(dm, dev, self.far.at[slot], self.frecv.at[slot])

    def swap(self):
        for dm in (3, 2, 1, 0):
            self.to_partner(dm).start()

    def add(self, dm, *more):
        dst = self.part.at[self.pos.blk(dm)]

        def body(rows):
            total = dst[rows, :].astype(F32) + self.prx[dm, rows, :].astype(F32)
            for ref in more:
                total = total + ref[rows, :].astype(F32)
            dst[rows, :] = total.astype(BF)

        row_loop(body)

    def outer_sends(self):
        p = self.pos

        @pl.when(p.outer())
        def _():
            for dm in (3, 2, 1):
                self.to_partner(dm).wait_recv()
                self.add(dm)
                self.hop_near(dm, p.away).start()

    def inner_step(self, i):
        p = self.pos

        @pl.when(p.inner())
        def _():
            if i == 1:
                self.to_partner(3).wait_recv()
                self.hop_near(3, p.away).wait_recv()
                self.add(3, self.near.at[2])
                self.hop_far(3, p.away, 0).start()
            if i == 2:
                self.to_partner(2).wait_recv()
                self.hop_near(2, p.away).wait_recv()
                self.add(2, self.near.at[1])
                self.hop_far(2, p.away, 1).start()
            if i == 3:
                self.to_partner(0).wait_recv()
                self.hop_far(0, p.near, 0).wait_recv()
                self.add(0, self.far.at[0])
                self.hop_far(0, p.near, 0).start()

    def final(self, use):
        p = self.pos

        @pl.when(p.outer())
        def _():
            self.to_partner(0).wait_recv()
            self.hop_far(0, p.near, 0).wait_recv()
            use((self.part.at[p.blk(0)], self.prx.at[0], self.far.at[0]))

        @pl.when(p.inner())
        def _():
            self.to_partner(1).wait_recv()
            self.hop_near(1, p.away).wait_recv()
            self.hop_far(1, p.away, 1).wait_recv()
            use((self.part.at[p.blk(1)], self.prx.at[1], self.near.at[0], self.far.at[1]))

    def drain(self):
        p = self.pos
        for dm in range(4):
            self.to_partner(dm).wait_send()

        @pl.when(p.outer())
        def _():
            for dm in (3, 2, 1):
                self.hop_near(dm, p.away).wait_send()

        @pl.when(p.inner())
        def _():
            for dm in (3, 2, 0):
                self.hop_far(dm, p.away, 0).wait_send()


def norm_value(wide, gain):
    inv_rms = lax.rsqrt(jnp.mean(wide * wide, axis=-1, keepdims=True) + NORM_EPS)
    return (wide * inv_rms * gain).astype(BF)


RELAY = 256
N_RELAY = REQ * OLD // RELAY


def qkv_kernel(pre_ref, x_ref, g_ref, bq_ref, bk_ref, bv_ref, kc_ref, vc_ref, wq_hbm, wk_hbm, wv_hbm,
               q_out, k_out, v_out, kn_out, vn_out, kh_out, vh_out,
               hbuf, wbuf, obuf, rbuf, cosb, sinb, cin, wide, cout,
               wsem, osem, rsem, isem, csem, gsend, grecv):
    pos = Place()
    weights = [pltpu.make_async_copy(src, wbuf.at[i], wsem.at[i]) for i, src in enumerate((wq_hbm, wk_hbm, wv_hbm))]
    for cp in weights:
        cp.start()
    gain = g_ref[...].astype(F32)
    gathers = [Gather(pos, hbuf.at[r], gsend.at[r], grecv.at[r]) for r in range(REQ)]

    per_req = OLD // RELAY
    srcs = (kc_ref, vc_ref)
    dsts = (kh_out, vh_out)

    def fetch(n, w, slot):
        return pltpu.make_async_copy(
            srcs[w].at[n // per_req, pl.ds(pl.multiple_of((n % per_req) * RELAY * HEADS, RELAY * HEADS), RELAY * HEADS)],
            cin.at[slot, w], isem.at[slot, w])

    def flush(n, w, slot):
        return pltpu.make_async_copy(
            cout.at[slot, w],
            dsts[w].at[n // per_req, :, pl.ds(pl.multiple_of((n % per_req) * RELAY, RELAY), RELAY)],
            csem.at[slot, w])

    for w in range(2):
        fetch(0, w, 0).start()

    def norm_rows(r):
        def body(rows):
            hbuf[r, pos.me, rows, :] = norm_value(x_ref[r, rows, :].astype(F32), gain)

        row_loop(body)

    norm_rows(0)
    entry_barrier(pos)
    gathers[0].start()
    norm_rows(1)
    gathers[1].start(inner=False)

    def relay(n, carry):
        slot = n % 2
        for w in range(2):
            @pl.when(n + 1 < N_RELAY)
            def _():
                fetch(n + 1, w, 1 - slot).start()

            fetch(n, w, slot).wait()

            @pl.when(n >= 2)
            def _():
                flush(n - 2, w, slot).wait()

            wide[w] = cin[slot, w].astype(F32)
            for h in range(HEADS):
                cout[slot, w, h] = wide[w, pl.ds(h, RELAY, stride=HEADS), :].astype(BF)
            flush(n, w, slot).start()
        return carry

    third = N_RELAY // 3
    lax.fori_loop(0, third, relay, 0)
    gathers[0].step(1)
    lax.fori_loop(third, 2 * third, relay, 0)
    gathers[0].step(2)
    gathers[1].start(outer=False)

    half = HD // 2
    lane = lax.broadcasted_iota(jnp.int32, (1, HD), 1)
    freq_id = (lane % half).astype(F32)
    inv_freq = jnp.exp((freq_id * 2.0 / HD) * (-jnp.log(jnp.float32(ROPE_THETA))))
    sign = jnp.where(lane < half, -1.0, 1.0).astype(F32)
    row_pos = lax.broadcasted_iota(jnp.int32, (CHUNK, 1), 0)
    for r in range(REQ):
        angles = (row_pos + pre_ref[r]).astype(F32) * inv_freq
        cosb[r] = jnp.cos(angles)
        sinb[r] = jnp.sin(angles) * sign

    lax.fori_loop(2 * third, N_RELAY, relay, 0)
    for n in (N_RELAY - 2, N_RELAY - 1):
        for w in range(2):
            flush(n, w, n % 2).wait()
    gathers[0].step(3)
    gathers[0].finish()
    for cp in weights:
        cp.wait()

    biases = (bq_ref, bk_ref, bv_ref)
    outs = (q_out, k_out, v_out)

    def head_out(i, r):
        return pltpu.make_async_copy(obuf.at[i, r], outs[i].at[r], osem.at[i, r])

    def row_out(i, r):
        return pltpu.make_async_copy(rbuf.at[i - 1, r], (kn_out, vn_out)[i - 1].at[r], rsem.at[i - 1, r])

    def project(i, r):
        for tile in range(2):
            cols = slice(tile * 256, tile * 256 + 256)
            acc = jnp.dot(hbuf[r].reshape(CHUNK, DIM), wbuf[i, :, cols], preferred_element_type=F32)
            val = (acc + biases[i][:, cols].astype(F32)).astype(BF)
            for k in range(2):
                h = tile * 2 + k
                head = val[:, k * HD:(k + 1) * HD]
                if i < 2:
                    wide_head = head.astype(F32)
                    head = (wide_head * cosb[r] + pltpu.roll(wide_head, half, 1) * sinb[r]).astype(BF)
                obuf[i, r, h] = head
                if i > 0:
                    rbuf[i - 1, r, :, h * HD:(h + 1) * HD] = head
        head_out(i, r).start()
        if i > 0:
            row_out(i, r).start()

    for i in range(3):
        project(i, 0)
        gathers[1].step(i + 1)
    gathers[1].finish()
    for i in range(3):
        project(i, 1)
    for r in range(REQ):
        gathers[r].drain()
        for i in range(3):
            head_out(i, r).wait()
            if i > 0:
                row_out(i, r).wait()


def run_qkv(x_rows, k_flat, v_flat, prefix, g, w_q, b_q, w_k, b_k, w_v, b_v):
    vm = pl.BlockSpec(memory_space=pltpu.VMEM)
    sm = pl.BlockSpec(memory_space=pltpu.SMEM)
    anyspace = pl.BlockSpec(memory_space=pl.ANY)
    head = jax.ShapeDtypeStruct((REQ, HEADS, CHUNK, HD), BF)
    rows = jax.ShapeDtypeStruct((REQ, CHUNK, HEADS * HD), BF)
    old = jax.ShapeDtypeStruct((REQ, HEADS, OLD, HD), BF)
    dma = pltpu.SemaphoreType.DMA
    return pl.pallas_call(
        qkv_kernel,
        out_shape=(head, head, head, rows, rows, old, old),
        in_specs=[sm, vm, vm, vm, vm, vm] + [anyspace] * 5,
        out_specs=[anyspace] * 7,
        scratch_shapes=[
            pltpu.VMEM((REQ, RANKS, ROWS, DIM), BF),
            pltpu.VMEM((3, DIM, HEADS * HD), BF),
            pltpu.VMEM((3, REQ, HEADS, CHUNK, HD), BF),
            pltpu.VMEM((2, REQ, CHUNK, HEADS * HD), BF),
            pltpu.VMEM((REQ, CHUNK, HD), F32),
            pltpu.VMEM((REQ, CHUNK, HD), F32),
            pltpu.VMEM((2, 2, RELAY * HEADS, HD), BF),
            pltpu.VMEM((2, RELAY * HEADS, HD), F32),
            pltpu.VMEM((2, 2, HEADS, RELAY, HD), BF),
            dma((3,)), dma((3, REQ)), dma((2, REQ)), dma((2, 2)), dma((2, 2)),
            dma((REQ, 9)), dma((REQ, RANKS)),
        ],
        compiler_params=pltpu.CompilerParams(collective_id=0, has_side_effects=True, vmem_limit_bytes=60 << 20),
        name="gather_qkv",
    )(prefix, x_rows, g.reshape(1, DIM), b_q.reshape(1, -1), b_k.reshape(1, -1), b_v.reshape(1, -1),
      k_flat, v_flat, w_q, w_k, w_v)


KB = 512
COPY = 512
N_COPY = REQ * SLOTS // COPY
STEPS = REQ * HEADS
PER_STEP = N_COPY // STEPS


def attn_kernel(pre_ref, val_ref, q_ref, ko_ref, vo_ref, kn_ref, vn_ref, kc_hbm, vc_hbm, krow_hbm, vrow_hbm,
                o_ref, kout_hbm, vout_hbm, cbuf, nbuf, isem, osem, nsem, usem):
    r = pl.program_id(0)
    h = pl.program_id(1)
    step = r * HEADS + h
    srcs = (kc_hbm, vc_hbm)
    dsts = (kout_hbm, vout_hbm)
    news = (krow_hbm, vrow_hbm)

    def chunk(s, j):
        n = s * PER_STEP + j
        return n // (SLOTS // COPY), pl.ds((n % (SLOTS // COPY)) * COPY, COPY)

    def take(s, j, w):
        i, rows = chunk(s, j)
        return pltpu.make_async_copy(srcs[w].at[i, rows], cbuf.at[s % 2, j, w], isem.at[s % 2, j, w])

    def put(s, j, w):
        i, rows = chunk(s, j)
        return pltpu.make_async_copy(cbuf.at[s % 2, j, w], dsts[w].at[i, rows], osem.at[s % 2, j, w])

    def each(fn):
        for j in range(PER_STEP):
            for w in range(2):
                fn(j, w)

    @pl.when(step == 0)
    def _():
        each(lambda j, w: take(0, j, w).start())
        for w in range(2):
            pltpu.make_async_copy(news[w], nbuf.at[w], nsem.at[w]).start()

    each(lambda j, w: take(step, j, w).wait())
    each(lambda j, w: put(step, j, w).start())

    @pl.when(step >= 1)
    def _():
        each(lambda j, w: put(step - 1, j, w).wait())

    @pl.when(step + 1 < STEPS)
    def _():
        each(lambda j, w: take(step + 1, j, w).start())

    p = pre_ref[r]
    c = val_ref[r]
    q = q_ref[0, 0]
    scale = (HD ** -0.5) * 1.4426950408889634

    def scores(keys):
        return lax.dot_general(q, keys, (((1,), (1,)), ((), ())), preferred_element_type=F32) * scale

    def fold(carry, s, vals):
        m, l, acc = carry
        m_new = jnp.maximum(m, jnp.max(s, axis=-1, keepdims=True))
        shrink = jnp.exp2(m - m_new)
        probs = jnp.exp2(s - m_new)
        l = l * shrink + jnp.sum(probs, axis=-1, keepdims=True)
        acc = acc * shrink + jnp.dot(probs.astype(BF), vals, preferred_element_type=F32)
        return m_new, l, acc

    rows = lax.broadcasted_iota(jnp.int32, (CHUNK, CHUNK), 0)
    cols = lax.broadcasted_iota(jnp.int32, (CHUNK, CHUNK), 1)
    s = jnp.where(cols <= jnp.minimum(rows, c - 1), scores(kn_ref[0, 0]), -1.0e30)
    m = jnp.max(s, axis=-1, keepdims=True)
    probs = jnp.exp2(s - m)
    l = jnp.sum(probs, axis=-1, keepdims=True)
    acc = jnp.dot(probs.astype(BF), vn_ref[0, 0], preferred_element_type=F32)

    def full(b, carry):
        rows = pl.ds(pl.multiple_of(b * KB, KB), KB)
        return fold(carry, scores(ko_ref[0, 0, rows, :]), vo_ref[0, 0, rows, :])

    def partial(b, carry):
        rows = pl.ds(pl.multiple_of(b * KB, KB), KB)
        s = jnp.where(cols + b * KB < p, scores(ko_ref[0, 0, rows, :]), -1.0e30)
        return fold(carry, s, vo_ref[0, 0, rows, :])

    n_full = p // KB
    n_all = (p + KB - 1) // KB
    carry = lax.fori_loop(0, n_full, full, (m, l, acc))
    m, l, acc = lax.fori_loop(n_full, n_all, partial, carry)
    o_ref[0] = (acc / l).astype(BF)

    @pl.when(step == STEPS - 1)
    def _():
        each(lambda j, w: put(step, j, w).wait())
        for w in range(2):
            pltpu.make_async_copy(news[w], nbuf.at[w], nsem.at[w]).wait()

        def updates(act):
            for i in range(REQ):
                n = val_ref[i]
                for bit in range(10):
                    size = 1 << bit
                    first = (n >> (bit + 1)) << (bit + 1)

                    @pl.when((n >> bit) % 2 == 1)
                    def _():
                        for w in range(2):
                            act(pltpu.make_async_copy(
                                nbuf.at[w, i, pl.ds(first, size)],
                                dsts[w].at[i, pl.ds(pre_ref[i] + first, size)],
                                usem.at[w, i, bit]))

        updates(lambda cp: cp.start())
        updates(lambda cp: cp.wait())


def run_attn(prefix, valid, q, k_old, v_old, k_new, v_new, k_cache, v_cache, k_rows, v_rows):
    def per_head(n):
        return pl.BlockSpec((1, 1, n, HD), lambda r, h, *_: (r, h, 0, 0))

    anyspace = pl.BlockSpec(memory_space=pl.ANY)
    dma = pltpu.SemaphoreType.DMA
    cache = jax.ShapeDtypeStruct((REQ, SLOTS, HEADS, HD), BF)
    return pl.pallas_call(
        attn_kernel,
        out_shape=(jax.ShapeDtypeStruct((REQ, CHUNK, HEADS * HD), BF), cache, cache),
        grid_spec=pltpu.PrefetchScalarGridSpec(
            num_scalar_prefetch=2,
            grid=(REQ, HEADS),
            in_specs=[per_head(CHUNK), per_head(OLD), per_head(OLD), per_head(CHUNK), per_head(CHUNK)] + [anyspace] * 4,
            out_specs=[pl.BlockSpec((1, CHUNK, HD), lambda r, h, *_: (r, 0, h)), anyspace, anyspace],
            scratch_shapes=[
                pltpu.VMEM((2, PER_STEP, 2, COPY, HEADS, HD), BF),
                pltpu.VMEM((2, REQ, CHUNK, HEADS, HD), BF),
                dma((2, PER_STEP, 2)), dma((2, PER_STEP, 2)), dma((2,)), dma((2, REQ, 10)),
            ],
        ),
        compiler_params=pltpu.CompilerParams(dimension_semantics=("arbitrary", "arbitrary"), vmem_limit_bytes=60 << 20),
        name="attend",
    )(prefix, valid, q, k_old, v_old, k_new, v_new, k_cache, v_cache, k_rows, v_rows)


FT = 256
N_FULL = FFN // FT
TAIL = FFN - N_FULL * FT
OT = 512


def mlp_kernel(x_ref, g_ref, o_hbm, wo_hbm, wg_hbm, wu_hbm, wd_hbm, out_ref,
               obuf, wo, wd, wgu, hbuf, ubuf, part, prx, near, far, mid,
               lsem, wsem, gsend, grecv, psend, precv, send, nrecv, frecv):
    pos = Place()
    loads = [pltpu.make_async_copy(src, dst, lsem.at[i]) for i, (src, dst) in enumerate(((o_hbm, obuf), (wo_hbm, wo), (wd_hbm, wd)))]
    for cp in loads:
        cp.start()

    def fetch(tile, slot, size):
        rows = pl.ds(pl.multiple_of(tile * FT, FT), size)
        return [pltpu.make_async_copy(src.at[rows], wgu.at[slot, w, pl.ds(0, size)], wsem.at[slot, w])
                for w, src in enumerate((wg_hbm, wu_hbm))]

    for cp in fetch(0, 0, FT):
        cp.start()
    gain = g_ref[...].astype(F32)
    gathers = [Gather(pos, hbuf.at[r], gsend.at[r], grecv.at[r]) for r in range(REQ)]
    scat = [[Scatter(pos, part.at[r], prx.at[r], near.at[r], far.at[r], psend.at[k, r], precv.at[k, r],
                     send.at[k, r], nrecv.at[k, r], frecv.at[k, r]) for r in range(REQ)] for k in range(2)]

    def into_part(r, lhs, weight):
        def tile(n, carry):
            cols = pl.ds(pl.multiple_of(n * OT, OT), OT)
            res = jnp.dot(lhs(), weight[:, cols], preferred_element_type=F32).astype(BF)
            part[r, :, :, cols] = res.reshape(RANKS, ROWS, OT)
            return carry

        lax.fori_loop(0, DIM // OT, tile, 0)

    def mid_rows(r):
        def use(refs):
            def body(rows):
                total = refs[0][rows, :].astype(F32)
                for ref in refs[1:]:
                    total = total + ref[rows, :].astype(F32)
                x1 = (x_ref[r, rows, :].astype(F32) + total.astype(BF).astype(F32)).astype(BF)
                mid[r, rows, :] = x1
                hbuf[r, pos.me, rows, :] = norm_value(x1.astype(F32), gain)

            row_loop(body)

        return use

    def out_rows(r):
        def use(refs):
            def body(rows):
                total = refs[0][rows, :].astype(F32)
                for ref in refs[1:]:
                    total = total + ref[rows, :].astype(F32)
                out_ref[r, rows, :] = (mid[r, rows, :].astype(F32) + total.astype(BF).astype(F32)).astype(BF)

            row_loop(body)

        return use

    def act(r, slot, size):
        dims = (((1,), (1,)), ((), ()))
        h = hbuf[r].reshape(CHUNK, DIM)
        gate = lax.dot_general(h, wgu[slot, 0, :size], dims, preferred_element_type=F32)
        up = lax.dot_general(h, wgu[slot, 1, :size], dims, preferred_element_type=F32)
        return (gate * (1.0 / (1.0 + jnp.exp(-gate))) * up).astype(BF)

    def mlp_up(r):
        def tile(n, carry):
            slot = n % 2
            for cp in fetch(n, slot, FT):
                cp.wait()

            @pl.when(n + 1 < N_FULL)
            def _():
                for cp in fetch(n + 1, 1 - slot, FT):
                    cp.start()

            @pl.when(n + 1 == N_FULL)
            def _():
                for cp in fetch(N_FULL, 1 - slot, TAIL):
                    cp.start()

            ubuf[:, pl.ds(pl.multiple_of(n * FT, FT), FT)] = act(r, slot, FT)
            return carry

        lax.fori_loop(0, N_FULL, tile, 0)
        slot = N_FULL % 2
        for cp in fetch(N_FULL, slot, TAIL):
            cp.wait()
        if r + 1 < REQ:
            for cp in fetch(0, 1 - slot, FT):
                cp.start()
        ubuf[:, N_FULL * FT:] = act(r, slot, TAIL)

    entry_barrier(pos)
    loads[0].wait()
    loads[1].wait()
    for r in range(REQ):
        into_part(r, lambda: obuf[r], wo)
        scat[0][r].swap()
        scat[0][r].outer_sends()
    for i in (1, 2, 3):
        scat[0][0].inner_step(i)
    scat[0][0].final(mid_rows(0))
    gathers[0].start()
    scat[0][1].inner_step(1)
    gathers[0].step(1)
    scat[0][1].inner_step(2)
    gathers[0].step(2)
    scat[0][1].inner_step(3)
    scat[0][1].final(mid_rows(1))
    gathers[0].step(3)
    gathers[1].start()
    gathers[0].finish()
    loads[2].wait()
    for r in range(REQ):
        mlp_up(r)
        if r == 0:
            gathers[1].step(1)
        gathers[r].drain()
        scat[0][r].drain()
        into_part(r, lambda: ubuf[...], wd)
        scat[1][r].swap()
        scat[1][r].outer_sends()
        if r == 0:
            gathers[1].step(2)
            gathers[1].step(3)
            gathers[1].finish()
            for i in (1, 2, 3):
                scat[1][0].inner_step(i)
    scat[1][0].final(out_rows(0))
    for i in (1, 2, 3):
        scat[1][1].inner_step(i)
    scat[1][1].final(out_rows(1))
    for r in range(REQ):
        scat[1][r].drain()


def run_mlp(x_rows, attended, g, w_o, w_gate_t, w_up_t, w_down):
    vm = pl.BlockSpec(memory_space=pltpu.VMEM)
    anyspace = pl.BlockSpec(memory_space=pl.ANY)
    dma = pltpu.SemaphoreType.DMA
    block = (ROWS, DIM)
    return pl.pallas_call(
        mlp_kernel,
        out_shape=jax.ShapeDtypeStruct((REQ, ROWS, DIM), BF),
        in_specs=[vm, vm] + [anyspace] * 5,
        out_specs=vm,
        scratch_shapes=[
            pltpu.VMEM((REQ, CHUNK, HEADS * HD), BF),
            pltpu.VMEM((HEADS * HD, DIM), BF),
            pltpu.VMEM((FFN, DIM), BF),
            pltpu.VMEM((2, 2, FT, DIM), BF),
            pltpu.VMEM((REQ, RANKS) + block, BF),
            pltpu.VMEM((CHUNK, FFN), BF),
            pltpu.VMEM((REQ, RANKS) + block, BF),
            pltpu.VMEM((REQ, 4) + block, BF),
            pltpu.VMEM((REQ, 3) + block, BF),
            pltpu.VMEM((REQ, 2) + block, BF),
            pltpu.VMEM((REQ,) + block, BF),
            dma((3,)), dma((2, 2)), dma((REQ, 9)), dma((REQ, RANKS)),
            dma((2, REQ, 4)), dma((2, REQ, 4)), dma((2, REQ, 4)), dma((2, REQ, 3)), dma((2, REQ, 2)),
        ],
        compiler_params=pltpu.CompilerParams(collective_id=1, has_side_effects=True, vmem_limit_bytes=63 << 20),
        name="out_mlp",
    )(x_rows, g.reshape(1, DIM), attended, w_o, w_gate_t, w_up_t, w_down)


def solution(mesh):
    row_spec = P("dp", "tp", None)
    cache_spec = P("dp", None, "tp", None)
    req_spec = P("dp")
    rep_spec = P(None)
    col_spec = P(None, "tp")
    bias_spec = P("tp")
    down_spec = P("tp", None)

    def layer(x_rows, k_cache, v_cache, prefix, valid, g_attn, w_q, b_q, w_k, b_k, w_v, b_v, w_o, g_mlp, w_gate, w_up, w_down):
        flat = (REQ, SLOTS * HEADS, HD)
        q, k_new, v_new, k_rows, v_rows, k_old, v_old = run_qkv(
            x_rows, k_cache.reshape(flat), v_cache.reshape(flat), prefix, g_attn, w_q, b_q, w_k, b_k, w_v, b_v)
        wide = (REQ, CHUNK, HEADS, HD)
        attended, k_out, v_out = run_attn(
            prefix, valid, q, k_old, v_old, k_new, v_new, k_cache, v_cache, k_rows.reshape(wide), v_rows.reshape(wide))
        x_out = run_mlp(x_rows, attended, g_mlp, w_o, w_gate.T, w_up.T, w_down)
        return x_out, k_out, v_out

    in_specs = (row_spec, cache_spec, cache_spec, req_spec, req_spec, rep_spec, col_spec, bias_spec, col_spec, bias_spec, col_spec, bias_spec, down_spec, rep_spec, col_spec, col_spec, down_spec)
    return jax.shard_map(layer, mesh=mesh, in_specs=in_specs, out_specs=(row_spec, cache_spec, cache_spec), check_vma=False)
```

time: 611 us -> 381 us (0.62); the launches traced: 600 us -> 382 us
  Pallas kernels: 0 us -> 369 us
  waiting for transfers between devices: 332 us -> 0 us
  matrix products: 148 us -> 0 us
  other arithmetic: 66.5 us -> 0 us
  local copies, waits for them, and re-layouts: 31.9 us -> 12.3 us
  between operations: 14.4 us -> 0.67 us
  loops' own time: 7.23 us -> 0 us
    pallas_call x0 -> x3, Pallas kernels: none -> 369 us  [the longest x1 232 us: run_mlp(): pl.pallas_call(mlp_kernel, out_shape=jax.ShapeDtypeStruct((REQ, ROWS, DIM...]
    reduce_scatter x2 -> x0, waiting for transfers between devices: 176 us -> none  [the longest x1 88.4 us: layer(): lax.psum_scatter(down_part, 'tp', scatter_dimension=1, tiled=True)]
    all_gather x2 -> x0, waiting for transfers between devices: 156 us -> none  [the longest x1 80.3 us: layer(): mlp_full = lax.all_gather(normed_mlp, 'tp', axis=1, tiled=True)]
    dot_general x9 -> x0, matrix products: 148 us -> none  [the longest x1 29.8 us: attend(): jnp.einsum('rkgcs,rskd->rckgd', attn_probs, v_cache, preferred_element_ty...]
    reduce_sum x3 -> x0, other arithmetic: 24.7 us -> none  [the longest x1 22.7 us: attend(): attn_probs = jax.nn.softmax(scores, axis=-1).astype(jnp.bfloat16)]
    unnamed x34 -> x3, local copies, waits for them, and re-layouts: 23.3 us -> 2.29 us
    dynamic_update_slice x4 -> x0, other arithmetic: 18.5 us -> none  [body(): return lax.dynamic_update_slice(buffer, merged, (req_idx, start, 0, 0))]
    reshape x0 -> x7, local copies, waits for them, and re-layouts: none -> 10 us  [the longest x1 2.17 us: layer(): v_rows.reshape(wide)]
  transfers between devices with their start and end apart: 4 -> 0, of which waited for: 4 -> 0; matrix products, arithmetic and copies ran while one was open for 1% -> 0% of each run, Pallas kernels for 0% -> 0%
where the time goes in v1:
time: 381 us; the launch traced here: 382 us
  Pallas kernels  369 us (97%)
  local copies, waits for them, and re-layouts  12.3 us (3%)
    pallas_call x1, Pallas kernels, run_mlp(): pl.pallas_call(mlp_kernel, out_shape=jax.ShapeDtypeStruct((REQ, ROWS, DIM...  232 us
    pallas_call x1, Pallas kernels, run_qkv(): pl.pallas_call(qkv_kernel, out_shape=(head, head, head, rows, rows, old,...  84.7 us
    pallas_call x1, Pallas kernels, run_attn(): pl.pallas_call(attn_kernel, out_shape=(jax.ShapeDtypeStruct((REQ, CHUNK,...  52.5 us

profile of v1, /device:TPU:0, one launch (start us, length us, event | category | flops | bytes accessed | tf_op | source)
XLA Modules:
  0.0 382.1 jit_solution(10742307226424417695)
XLA Ops:
  0.6 1.3 reshape.34.g_ref
  1.9 1.3 reshape.35.bq_ref
  3.2 1.3 reshape.36.bk_ref
  4.5 1.3 reshape.37.bv_ref
  5.7 84.7 %gather_qkv.1 = (bf16[2,4,512,128]{3,2,1,0:T(8,128)(2,1)}, bf16[2,4,512,128]{3,2,1,0:T(8,128)(2,1)}, bf16[2,4,512,128]{3,2,1,0:T(8,128)(2,1)}, bf16[2,512,512]{2...) custom-call(s32[2]{0:T(128)} %pre_ref.3, ...), custom_call_target="tpu_custom_call" | custom-call | tf_op jit(solution)/shard_map/gather_qkv/pallas_call | solution.py:401
  90.5 2.1 reshape.40.krow_hbm
  92.6 2.2 reshape.41.vrow_hbm
  94.8 0.0 copy-start
  94.8 52.5 %attend.1 = (bf16[2,512,512]{2,1,0:T(8,128)(2,1)}, bf16[2,4096,4,128]{3,2,1,0:T(4,128)(2,1)}, bf16[2,4096,4,128]{3,2,1,0:T(4,128)(2,1)}) custom-call(s32[2]{0:T(128)} %pre_ref.3, s32[2]{0:T(128)} %val_ref.1, bf16[2,4,512,128]{3,2,1,0:T(8,128)(2,1)} %get-tuple-element.13.q_ref, bf16[2,4,3584,128]{3,2,1,0:T(8,128)(2,1)} %get-tuple-element.14.ko_ref, ...), custom_call_target="tpu_custom_call" | custom-call | tf_op jit(solution)/shard_map/attend/pallas_call | solution.py:547
  147.3 0.0 copy-done
  147.3 0.6 reshape.33.g_ref
  147.9 231.9 %out_mlp.1 = bf16[2,64,4096]{2,1,0:T(8,128)(2,1)} custom-call(bf16[2,64,4096]{2,1,0:T(8,128)(2,1)} %x_ref.3, bf16[1,4096]{1,0:T(2,128)(2,1)} %reshape.33.g_ref, bf16[2,512,512]{2,1,0:T(8,128)(2,1)} %get-tuple-element.20.o_hbm, bf16[512,4096]{1,0:T(8,128)(2,1)} %wo_hbm.1, bf16[1376,4096]{1,0:T(8,128)(2,1)} %bitcast.6, bf16[1376,4096]{1,0:T(8,128)(2,1)} %bitcast.7, ...), custom_call_target="tpu_custom_call" | custom-call | tf_op jit(solution)/shard_map/out_mlp/pallas_call | solution.py:711
  379.8 2.3 copy.21
Async XLA Ops:
  94.8 52.5 %copy-start = (bf16[4096]{0:T(1024)(128)(2,1)S(1)}, bf16[4096]{0:T(1024)(128)(2,1)}, u32[]{:S(2)}) copy-start(bf16[4096]{0:T(1024)(128)(2,1)} %param.30) | copy-start | bytes 24580
